TPU v7x, 32 devices: a whole 2x2x4 slice. The times are simulated.
32 devices in a mesh: dp: 8 (over y, x, core), mp: 4 (over z).
Axes of the slice: x: 2, y: 2, z: 4, core: 2. Of those that a mesh axis runs over, the one named last changes fastest.
Arguments:
- tokens: bfloat16 [8192, 2048], P('dp'), may hold values from -6 to 6
- doc_ids: int32 [16, 512], P('dp'), may hold values from 0 to 3, never falling along the last dimension, each value on 1 to 256 neighbouring positions
- selection: int32 [16, 512], P('dp'), may hold values 0 or 1
- w_query: bfloat16 [2048, 2048], P('dp', 'mp'), may hold values from -0.125 to 0.125
- w_key: bfloat16 [2048, 256], P('dp', 'mp'), may hold values from -0.125 to 0.125
- w_value: bfloat16 [2048, 256], P('dp', 'mp'), may hold values from -0.125 to 0.125
- w_out: bfloat16 [2048, 2048], P('mp', 'dp'), may hold values from -0.375 to 0.375
- w_gate: bfloat16 [2048, 5632], P('dp', 'mp'), may hold values from -0.125 to 0.125
- w_up: bfloat16 [2048, 5632], P('dp', 'mp'), may hold values from -0.125 to 0.125
- w_down: bfloat16 [5632, 2048], P('mp', 'dp'), may hold values from -0.078125 to 0.078125
- attn_gain: bfloat16 [2048], P('dp'), may hold values from 0.25 to 1.75
- mlp_gain: bfloat16 [2048], P('dp'), may hold values from 0.25 to 1.75
- cotangent: bfloat16 [8192, 2048], P('dp'), may hold values from -6 to 6
Outputs:
- output: bfloat16 [8192, 2048], P('dp')
- input_grad: float32 [8192, 2048], P('dp')
- grad_w_query: float32 [2048, 2048], P('dp', 'mp')
- grad_w_key: float32 [2048, 256], P('dp', 'mp')
- grad_w_value: float32 [2048, 256], P('dp', 'mp')
- grad_w_out: float32 [2048, 2048], P('mp', 'dp')
- grad_w_gate: float32 [2048, 5632], P('dp', 'mp')
- grad_w_up: float32 [2048, 5632], P('dp', 'mp')
- grad_w_down: float32 [5632, 2048], P('mp', 'dp')
- grad_attn_gain: float32 [2048], P('dp')
- grad_mlp_gain: float32 [2048], P('dp')
Inputs may be any that keep to these rules, and one draw needn't show every extreme that they name: `doc_ids`: within a sequence the ids never fall; a document spans 1 to 256 tokens and one spans exactly 256.
All inputs are finite; a program needn't handle non-finite values. No bound on the sum of `selection` on one device may be relied on, other than what follows from the above.
Results may differ from a plain program's by a relative error of at most 0.024.
Values may be sent and summed in bfloat16 or wider, within the bound.
A program may use at most 256 MiB of HBM per device.

v0:
```python
import jax
import jax.numpy as jnp
from jax import lax
from jax.sharding import PartitionSpec as P

HEAD_DIM = 64
EPSILON = 1e-05
MASKED = -1e30


def rope_tables(length, head_width):
    half_width = head_width // 2
    frequency = 10000.0 ** (-2.0 * jnp.arange(half_width, dtype=jnp.float32) / head_width)
    places = jnp.arange(length, dtype=jnp.float32)
    angles = places[:, None] * frequency[None, :]
    return (jnp.cos(angles)[:, None, :], jnp.sin(angles)[:, None, :])


def rotate(field, cosine_table, sine_table):
    half_width = field.shape[-1] // 2
    first_half = field[..., :half_width]
    second_half = field[..., half_width:]
    return jnp.concatenate(
        [
            first_half * cosine_table - second_half * sine_table,
            second_half * cosine_table + first_half * sine_table,
        ],
        axis=-1,
    )


def allowed_pairs(doc_row):
    length = doc_row.shape[0]
    query_index = lax.broadcasted_iota(jnp.int32, (length, length), 0)
    key_index = lax.broadcasted_iota(jnp.int32, (length, length), 1)
    return (doc_row[:, None] == doc_row[None, :]) & (query_index >= key_index)


def rms_forward(residual, gain_row):
    inverse = lax.rsqrt(jnp.mean(residual * residual, axis=-1, keepdims=True) + EPSILON)
    return (residual * inverse * gain_row, inverse)


def rms_backward(residual, inverse, gain_row, grad_normed):
    scaled = grad_normed * gain_row
    gain_part = jnp.sum(grad_normed * residual * inverse, axis=0)
    mean_term = jnp.mean(scaled * residual, axis=-1, keepdims=True)
    return (inverse * scaled - residual * (inverse * inverse * inverse) * mean_term, gain_part)


def attend_forward(queries, key_rows, value_rows, doc_row, score_scale):
    length, kv_local, head_width = key_rows.shape
    grouped = queries.reshape(length, kv_local, -1, head_width)
    scores = (
        jnp.einsum("qkgd,skd->kgqs", grouped, key_rows, preferred_element_type=jnp.float32)
        * score_scale
    )
    scores = jnp.where(allowed_pairs(doc_row), scores, MASKED)
    highest = jnp.max(scores, axis=-1, keepdims=True)
    shifted_exp = jnp.exp(scores - highest)
    totals = jnp.sum(shifted_exp, axis=-1, keepdims=True)
    probs_low = (shifted_exp / totals).astype(jnp.bfloat16)
    mixed_heads = jnp.einsum(
        "kgqs,skd->qkgd", probs_low, value_rows, preferred_element_type=jnp.float32
    )
    return (mixed_heads.reshape(length, -1), highest + jnp.log(totals))


def attend_backward(queries, key_rows, value_rows, doc_row, logsum, grad_mixed, score_scale):
    length, kv_local, head_width = key_rows.shape
    grouped = queries.reshape(length, kv_local, -1, head_width)
    grad_grouped = grad_mixed.reshape(length, kv_local, -1, head_width)
    scores = (
        jnp.einsum("qkgd,skd->kgqs", grouped, key_rows, preferred_element_type=jnp.float32)
        * score_scale
    )
    attn_probs = jnp.where(allowed_pairs(doc_row), jnp.exp(scores - logsum), 0.0)
    grad_probs = jnp.einsum(
        "qkgd,skd->kgqs", grad_grouped, value_rows, preferred_element_type=jnp.float32
    )
    inner_sum = jnp.sum(attn_probs * grad_probs, axis=-1, keepdims=True)
    grad_scores = (attn_probs * (grad_probs - inner_sum)).astype(jnp.bfloat16)
    grad_queries = (
        jnp.einsum("kgqs,skd->qkgd", grad_scores, key_rows, preferred_element_type=jnp.float32)
        * score_scale
    )
    grad_keys = (
        jnp.einsum("kgqs,qkgd->skd", grad_scores, grouped, preferred_element_type=jnp.float32)
        * score_scale
    )
    grad_values = jnp.einsum(
        "kgqs,qkgd->skd",
        attn_probs.astype(jnp.bfloat16),
        grad_grouped,
        preferred_element_type=jnp.float32,
    )
    return (grad_queries.reshape(length, -1, head_width), grad_keys, grad_values)


def per_device(
    tokens,
    doc_ids,
    selection,
    w_query,
    w_key,
    w_value,
    w_out,
    w_gate,
    w_up,
    w_down,
    attn_gain,
    mlp_gain,
    cotangent,
):
    (
        full_query,
        full_key,
        full_value,
        full_out,
        full_gate,
        full_up,
        full_down,
        gathered_one,
        gathered_two,
    ) = (
        lax.all_gather(w_query, "dp", axis=0, tiled=True),
        lax.all_gather(w_key, "dp", axis=0, tiled=True),
        lax.all_gather(w_value, "dp", axis=0, tiled=True),
        lax.all_gather(w_out, "dp", axis=1, tiled=True),
        lax.all_gather(w_gate, "dp", axis=0, tiled=True),
        lax.all_gather(w_up, "dp", axis=0, tiled=True),
        lax.all_gather(w_down, "dp", axis=1, tiled=True),
        lax.all_gather(attn_gain, "dp", axis=0, tiled=True),
        lax.all_gather(mlp_gain, "dp", axis=0, tiled=True),
    )
    gain_one = gathered_one.astype(jnp.float32)
    gain_two = gathered_two.astype(jnp.float32)
    seq_local, length = doc_ids.shape
    tok_local = seq_local * length
    heads_local = full_query.shape[1] // HEAD_DIM
    kv_local = full_key.shape[1] // HEAD_DIM
    score_scale = HEAD_DIM ** (-0.5)
    cosine_table, sine_table = rope_tables(length, HEAD_DIM)
    residual = tokens.astype(jnp.float32)
    normed_float, inverse_one = rms_forward(residual, gain_one)
    normed_one = normed_float.astype(jnp.bfloat16)
    query_lin = jnp.dot(normed_one, full_query, preferred_element_type=jnp.float32).reshape(
        seq_local, length, heads_local, HEAD_DIM
    )
    key_lin = jnp.dot(normed_one, full_key, preferred_element_type=jnp.float32).reshape(
        seq_local, length, kv_local, HEAD_DIM
    )
    value_rows = (
        jnp.dot(normed_one, full_value, preferred_element_type=jnp.float32)
        .astype(jnp.bfloat16)
        .reshape(seq_local, length, kv_local, HEAD_DIM)
    )
    query_rot = rotate(query_lin, cosine_table, sine_table).astype(jnp.bfloat16)
    key_rot = rotate(key_lin, cosine_table, sine_table).astype(jnp.bfloat16)

    def forward_one(bundle):
        return attend_forward(bundle[0], bundle[1], bundle[2], bundle[3], score_scale)

    mixed_heads, logsum = lax.map(forward_one, (query_rot, key_rot, value_rows, doc_ids))
    mixed_low = mixed_heads.reshape(tok_local, heads_local * HEAD_DIM).astype(jnp.bfloat16)
    attn_partial = jnp.dot(mixed_low, full_out, preferred_element_type=jnp.float32)
    hidden_in = residual + lax.psum(attn_partial.astype(jnp.bfloat16), "mp").astype(jnp.float32)
    normed_two_float, inverse_two = rms_forward(hidden_in, gain_two)
    normed_two = normed_two_float.astype(jnp.bfloat16)
    gate_lin = jnp.dot(normed_two, full_gate, preferred_element_type=jnp.float32)
    up_lin = jnp.dot(normed_two, full_up, preferred_element_type=jnp.float32)
    sig_gate = jax.nn.sigmoid(gate_lin)
    swish_gate = gate_lin * sig_gate
    hidden = (swish_gate * up_lin).astype(jnp.bfloat16)
    mlp_partial = jnp.dot(hidden, full_down, preferred_element_type=jnp.float32)
    output = (
        hidden_in + lax.psum(mlp_partial.astype(jnp.bfloat16), "mp").astype(jnp.float32)
    ).astype(jnp.bfloat16)
    grad_y = cotangent.astype(jnp.float32) * selection.reshape(tok_local, 1).astype(jnp.float32)
    grad_y_low = grad_y.astype(jnp.bfloat16)
    grad_down = jnp.einsum("tf,td->fd", hidden, grad_y_low, preferred_element_type=jnp.float32)
    grad_hidden = jnp.einsum("td,fd->tf", grad_y_low, full_down, preferred_element_type=jnp.float32)
    grad_gate_low = (grad_hidden * up_lin * sig_gate * (1.0 + gate_lin * (1.0 - sig_gate))).astype(
        jnp.bfloat16
    )
    grad_up_low = (grad_hidden * swish_gate).astype(jnp.bfloat16)
    grad_gate_w = jnp.einsum(
        "td,tf->df", normed_two, grad_gate_low, preferred_element_type=jnp.float32
    )
    grad_up_w = jnp.einsum("td,tf->df", normed_two, grad_up_low, preferred_element_type=jnp.float32)
    partial_two = jnp.einsum(
        "tf,df->td", grad_gate_low, full_gate, preferred_element_type=jnp.float32
    ) + jnp.einsum("tf,df->td", grad_up_low, full_up, preferred_element_type=jnp.float32)
    grad_normed_two = lax.psum(partial_two.astype(jnp.bfloat16), "mp").astype(jnp.float32)
    grad_resid_two, gain_grad_two = rms_backward(hidden_in, inverse_two, gain_two, grad_normed_two)
    grad_h = grad_y + grad_resid_two
    grad_h_low = grad_h.astype(jnp.bfloat16)
    grad_out_w = jnp.einsum("tc,td->cd", mixed_low, grad_h_low, preferred_element_type=jnp.float32)
    grad_mixed = jnp.einsum(
        "td,cd->tc", grad_h_low, full_out, preferred_element_type=jnp.float32
    ).astype(jnp.bfloat16)
    grad_mixed = grad_mixed.reshape(seq_local, length, heads_local * HEAD_DIM)

    def backward_one(bundle):
        return attend_backward(
            bundle[0], bundle[1], bundle[2], bundle[3], bundle[4], bundle[5], score_scale
        )

    grad_query_rot, grad_key_rot, grad_values = lax.map(
        backward_one, (query_rot, key_rot, value_rows, doc_ids, logsum, grad_mixed)
    )
    grad_query_lin = (
        rotate(grad_query_rot, cosine_table, -sine_table)
        .reshape(tok_local, heads_local * HEAD_DIM)
        .astype(jnp.bfloat16)
    )
    grad_key_lin = (
        rotate(grad_key_rot, cosine_table, -sine_table)
        .reshape(tok_local, kv_local * HEAD_DIM)
        .astype(jnp.bfloat16)
    )
    grad_value_low = grad_values.reshape(tok_local, kv_local * HEAD_DIM).astype(jnp.bfloat16)
    grad_query_w = jnp.einsum(
        "td,tc->dc", normed_one, grad_query_lin, preferred_element_type=jnp.float32
    )
    grad_key_w = jnp.einsum(
        "td,tc->dc", normed_one, grad_key_lin, preferred_element_type=jnp.float32
    )
    grad_value_w = jnp.einsum(
        "td,tc->dc", normed_one, grad_value_low, preferred_element_type=jnp.float32
    )
    partial_one = (
        jnp.einsum("tc,dc->td", grad_query_lin, full_query, preferred_element_type=jnp.float32)
        + jnp.einsum("tc,dc->td", grad_key_lin, full_key, preferred_element_type=jnp.float32)
        + jnp.einsum("tc,dc->td", grad_value_low, full_value, preferred_element_type=jnp.float32)
    )
    grad_normed_one = lax.psum(partial_one.astype(jnp.bfloat16), "mp").astype(jnp.float32)
    grad_resid_one, gain_grad_one = rms_backward(residual, inverse_one, gain_one, grad_normed_one)
    input_grad = grad_h + grad_resid_one
    (
        shard_query,
        shard_key,
        shard_value,
        shard_out,
        shard_gate,
        shard_up,
        shard_down,
        shard_gain_one,
        shard_gain_two,
    ) = (
        lax.psum_scatter(
            grad_query_w.astype(jnp.bfloat16), "dp", scatter_dimension=0, tiled=True
        ).astype(jnp.float32),
        lax.psum_scatter(
            grad_key_w.astype(jnp.bfloat16), "dp", scatter_dimension=0, tiled=True
        ).astype(jnp.float32),
        lax.psum_scatter(
            grad_value_w.astype(jnp.bfloat16), "dp", scatter_dimension=0, tiled=True
        ).astype(jnp.float32),
        lax.psum_scatter(
            grad_out_w.astype(jnp.bfloat16), "dp", scatter_dimension=1, tiled=True
        ).astype(jnp.float32),
        lax.psum_scatter(
            grad_gate_w.astype(jnp.bfloat16), "dp", scatter_dimension=0, tiled=True
        ).astype(jnp.float32),
        lax.psum_scatter(
            grad_up_w.astype(jnp.bfloat16), "dp", scatter_dimension=0, tiled=True
        ).astype(jnp.float32),
        lax.psum_scatter(
            grad_down.astype(jnp.bfloat16), "dp", scatter_dimension=1, tiled=True
        ).astype(jnp.float32),
        lax.psum_scatter(
            gain_grad_one.astype(jnp.bfloat16), "dp", scatter_dimension=0, tiled=True
        ).astype(jnp.float32),
        lax.psum_scatter(
            gain_grad_two.astype(jnp.bfloat16), "dp", scatter_dimension=0, tiled=True
        ).astype(jnp.float32),
    )
    return (
        output,
        input_grad,
        shard_query,
        shard_key,
        shard_value,
        shard_out,
        shard_gate,
        shard_up,
        shard_down,
        shard_gain_one,
        shard_gain_two,
    )


def solution(mesh):
    in_specs = (
        P("dp", None),
        P("dp", None),
        P("dp", None),
        P("dp", "mp"),
        P("dp", "mp"),
        P("dp", "mp"),
        P("mp", "dp"),
        P("dp", "mp"),
        P("dp", "mp"),
        P("mp", "dp"),
        P("dp"),
        P("dp"),
        P("dp", None),
    )
    out_specs = (
        P("dp", None),
        P("dp", None),
        P("dp", "mp"),
        P("dp", "mp"),
        P("dp", "mp"),
        P("mp", "dp"),
        P("dp", "mp"),
        P("dp", "mp"),
        P("mp", "dp"),
        P("dp"),
        P("dp"),
    )
    return jax.shard_map(
        per_device, mesh=mesh, in_specs=in_specs, out_specs=out_specs, check_vma=False
    )
```

profile of v0, /device:TPU:0, one launch (start us, length us, event | category | flops | bytes accessed | tf_op | source)
XLA Modules:
  0.0 1349.3 jit_solution(685220449423602048)
XLA Ops:
  9.6 3.2 fusion.66
  13.4 10.4 all-gather
  24.8 10.8 all_gather.29
  35.6 9.4 all_gather.28
  49.5 3.7 fusion.88
  53.6 6.6 fusion.89
  60.2 4.2 reshape.285
  68.6 15.0 %while.26 = (s32[]{:T(128)}, bf16[2,512,512]{2,1,0:T(8,128)(2,1)S(1)}, f32[2,1,8,512,1]{3,2,4,1,0:T(8,128)}, bf16[2,512,1,64]{1,3,2,0:T(8,128)(2,1)S(1)}, s32[2,...) while((s32[]{:T(128)}, ...), condition=%wide.region_4.5_spmd, body=%wide.region_1.4_spmd.sunk | while | flops 562819072 | bytes 29629548 | solution.py:164
  83.7 6.3 convolution_convert_fusion.4
  91.9 8.8 all-gather.1
  100.7 144.7 %all-reduce.8.cloned.1.call-done = bf16[1024,2048]{1,0:T(8,128)(2,1)} async-done(((bf16[1024,2048]{1,0:T(8,128)(2,1)}), bf16[1024,2048]{1,0:T(8,128)(2,1)}) %all-reduce.8.cloned.1.call-update) | async-done | bytes 4194320 | tf_op jit(solution)/shard_map/psum | solution.py:167
  245.4 5.0 multiply_reduce_fusion
  251.3 4.0 multiply_convert_fusion
  255.4 34.0 %all-gather.14.cloned.1.call-done = bf16[2048,1408]{1,0:T(8,128)(2,1)} async-done(((bf16[256,1408]{1,0:T(8,128)(2,1)}), bf16[2048,1408]{1,0:T(8,128)(2,1)}) %all-gather.14.cloned.1.call-update) | async-done | bytes 5767184 | tf_op jit(solution)/shard_map/all_gather | solution.py:131
  289.3 11.7 fusion.91
  301.0 33.3 %all-gather.12.cloned.1.call-done = bf16[2048,1408]{1,0:T(8,128)(2,1)} async-done(((bf16[256,1408]{1,0:T(8,128)(2,1)}), bf16[2048,1408]{1,0:T(8,128)(2,1)}) %all-gather.12.cloned.1.call-update) | async-done | bytes 5767184 | tf_op jit(solution)/shard_map/all_gather | solution.py:130
  334.3 11.7 fusion.90
  346.0 34.3 %all-gather.16.cloned.1.call-done = bf16[1408,2048]{1,0:T(8,128)(2,1)} async-done(((bf16[1408,256]{1,0:T(8,128)(2,1)}), bf16[1408,2048]{1,0:T(8,128)(2,1)}) %all-gather.16.cloned.1.call-update) | async-done | bytes 5767184 | tf_op jit(solution)/shard_map/all_gather | solution.py:132
  380.3 17.0 %multiply_convert_fusion.1 = (bf16[1024,1408]{1,0:T(8,128)(2,1)}, bf16[1024,1408]{1,0:T(8,128)(2,1)}, bf16[1024,1408]{1,0:T(8,128)(2,1)}) fusion(f32[1024,1408]{1,0:T(8,128)} %fusion.90, f32[1024,1408]{1,0:T(8,128)} %fusion.91, bf16[1408,2048]{1,0:T(8,128)(2,1)} %all-gather.16.cloned.1.call-done, bf16[1024,2048]{1,0:T(8,128)(2,1)} %param.29, ...), kind=kOutput, calls=%fused_computation.103 | convolution fusion | flops 5933498368 | bytes 30150656 | tf_op jit(solution)/shard_map/td,fd->tf/dot_general | solution.py:182
  397.3 8.7 fusion.92
  406.0 11.0 add_convert_fusion.1
  417.1 155.1 %all-reduce.10.cloned.1.call-done = bf16[1024,2048]{1,0:T(8,128)(2,1)} async-done(((bf16[1024,2048]{1,0:T(8,128)(2,1)}), bf16[1024,2048]{1,0:T(8,128)(2,1)}) %all-reduce.10.cloned.1.call-update) | async-done | bytes 4194320 | tf_op jit(solution)/shard_map/psum | solution.py:194
  572.1 8.6 fusion.65
  580.7 6.1 fusion.62
  590.2 70.1 %while.27 = (s32[]{:T(128)}, f32[2,512,8,64]{1,0,3,2:T(2,128)}, f32[2,512,1,64]{1,3,2,0:T(8,128)}, bf16[2,512,1,64]{1,3,2,0:T(8,128)(2,1)}, bf16[2,512,1,64]{1,3...) while((s32[]{:T(128)}, f32[2,512,8,64]{1,0,3,2:T(2,128)}, ...), condition=%wide.region_12.13_spmd, body=%wide.region_10.12_spmd.sunk | while | flops 1374711808 | bytes 77127944 | solution.py:209
  596.3 2.8 fusion.176
  599.1 2.7 fusion.177
  605.9 19.6 %dynamic_update_slice.32 = f32[2,512,8,64]{1,0,3,2:T(2,128)} dynamic-update-slice(f32[2,512,8,64]{1,0,3,2:T(2,128)} %get-tuple-element.378, f32[1,512,8,64]{1,0,3,2:T(1,128)S(1)} %copy.100, s32[]{:T(128)S(6)} %copy.121, s32[]{:T(128)} %constant.66.clone.1..sunk, s32[]{:T(128)} %constant.66.clone.1..sunk, s32[]{:T(128)} %constant.66.clone.1..sunk) | dynamic-update-slice | bytes 2097156 | tf_op jit(solution)/shard_map/while/body/jit(dynamic_update_index_in_dim)/dynamic_update_slice | solution.py:209
  631.2 2.8 fusion.176
  640.7 19.6 %dynamic_update_slice.32 = f32[2,512,8,64]{1,0,3,2:T(2,128)} dynamic-update-slice(f32[2,512,8,64]{1,0,3,2:T(2,128)} %get-tuple-element.378, f32[1,512,8,64]{1,0,3,2:T(1,128)S(1)} %copy.100, s32[]{:T(128)S(6)} %copy.121, s32[]{:T(128)} %constant.66.clone.1..sunk, s32[]{:T(128)} %constant.66.clone.1..sunk, s32[]{:T(128)} %constant.66.clone.1..sunk) | dynamic-update-slice | bytes 2097156 | tf_op jit(solution)/shard_map/while/body/jit(dynamic_update_index_in_dim)/dynamic_update_slice | solution.py:209
  664.2 3.7 convolution_convert_fusion.8
  670.9 3.8 convolution_convert_fusion.7
  674.7 6.0 convolution_convert_fusion.6
  680.9 7.1 convolution_convert_fusion.5
  688.0 11.0 convolution_convert_fusion.1
  699.1 11.0 convolution_convert_fusion.2
  710.7 10.9 convolution_convert_fusion
  721.9 10.9 convolution_convert_fusion.3
  736.8 3.2 add_convert_fusion
  744.7 37.6 %reduce-scatter.8.cloned.1.call-done = bf16[256,512]{1,0:T(8,128)(2,1)} async-done(((bf16[2048,512]{1,0:T(8,128)(2,1)}), bf16[256,512]{1,0:T(8,128)(2,1)}) %reduce-scatter.8.cloned.1.call-update) | async-done | bytes 262160 | tf_op jit(solution)/shard_map/reduce_scatter | solution.py:251
  784.1 42.6 %reduce-scatter.14.cloned.1.call-done = bf16[512,256]{1,0:T(8,128)(2,1)} async-done(((bf16[512,2048]{1,0:T(8,128)(2,1)}), bf16[512,256]{1,0:T(8,128)(2,1)}) %reduce-scatter.14.cloned.1.call-update) | async-done | bytes 262160 | tf_op jit(solution)/shard_map/reduce_scatter | solution.py:260
  828.6 60.6 %reduce-scatter.18.cloned.1.call-done = bf16[256,1408]{1,0:T(8,128)(2,1)} async-done(((bf16[2048,1408]{1,0:T(8,128)(2,1)}), bf16[256,1408]{1,0:T(8,128)(2,1)}) %reduce-scatter.18.cloned.1.call-update) | async-done | bytes 720912 | tf_op jit(solution)/shard_map/reduce_scatter | solution.py:266
  891.4 60.2 %reduce-scatter.16.cloned.1.call-done = bf16[256,1408]{1,0:T(8,128)(2,1)} async-done(((bf16[2048,1408]{1,0:T(8,128)(2,1)}), bf16[256,1408]{1,0:T(8,128)(2,1)}) %reduce-scatter.16.cloned.1.call-update) | async-done | bytes 720912 | tf_op jit(solution)/shard_map/reduce_scatter | solution.py:263
  954.0 59.9 %reduce-scatter.20.cloned.1.call-done = bf16[1408,256]{1,0:T(8,128)(2,1)} async-done(((bf16[1408,2048]{1,0:T(8,128)(2,1)}), bf16[1408,256]{1,0:T(8,128)(2,1)}) %reduce-scatter.20.cloned.1.call-update) | async-done | bytes 720912 | tf_op jit(solution)/shard_map/reduce_scatter | solution.py:269
  1016.2 291.6 %all-reduce.12.cloned.1.call-done = (bf16[1024,2048]{1,0:T(8,128)(2,1)}, bf16[1024,2048]{1,0:T(8,128)(2,1)}) async-done(((bf16[1024,2048]{1,0:T(8,128)(2,1)}, bf16[1024,2048]{1,0:T(8,128)(2,1)}), (bf16[1024,2048]{1,0:T(8,128)(2,1)}, bf16[1024,2048]{1,0:T(8,128)(2,1)})) %all-reduce.12.cloned.1.call-update) | async-done | bytes 8388624 | tf_op jit(solution)/shard_map/psum | solution.py:177
  1307.8 5.6 fusion.72
  1313.4 13.7 %all-reduce.2 = (bf16[2048]{0:T(1024)(128)(2,1)S(1)}, bf16[2048]{0:T(1024)(128)(2,1)S(1)}) all-reduce(bf16[2048]{0:T(1024)(128)(2,1)S(1)} %get-tuple-element.161, bf16[2048]{0:T(1024)(128)(2,1)S(1)} %copy-done.24), channel_id=9, replica_groups=mesh['dp'=8,'mp'=4] {'dp'}, use_global_device_ids=true, to_apply=%region_23.24.clone | all-reduce | flops 4096 | bytes 16384
  1327.8 14.6 %fusion.60 = (f32[1024,2048]{1,0:T(8,128)}, bf16[1024,2048]{1,0:T(8,128)(2,1)}) fusion(f32[1024,2048]{1,0:T(8,128)} %copy-done.6, bf16[1024,2048]{1,0:T(8,128)(2,1)} %get-tuple-element.200, bf16[1024,2048]{1,0:T(8,128)(2,1)} %param.17, f32[1024]{0:T(1024)S(1)} %broadcast_multiply_fusion, f32[1024]{0:T(1024)S(1)} %copy-done.23, f32[2048]{0:T(1024)S(1)} %bitcast.299, ...), kind=kLoop, calls=%fused_computation.80 | loop fusion | flops 27262976 | bytes 37769216 | tf_op jit(solution)/shard_map/add | solution.py:239
  (196 shorter events, 83.1 us)
Async XLA Ops:
  7.2 46.4 %all-gather.8.cloned.1.call-start = ((), (), s32[]{:S(2)}) async-start(), calls=%async_computation.7 | async-start | bytes 2359296 | tf_op jit(solution)/shard_map/all_gather | solution.py:126
  7.9 75.8 %all-gather.10.cloned.1.call-start = ((), (), s32[]{:S(2)}) async-start(), calls=%async_computation.8 | async-start | bytes 2359296 | tf_op jit(solution)/shard_map/all_gather | solution.py:129
  8.7 236.7 %all-reduce.8.cloned.1.call-start = ((), (), s32[]{:S(2)}) async-start(), calls=%async_computation.9 | async-start | bytes 8388608 | tf_op jit(solution)/shard_map/psum | solution.py:167
  8.7 36.2 %copy-start = (bf16[1024,2048]{1,0:T(8,128)(2,1)S(1)}, bf16[1024,2048]{1,0:T(8,128)(2,1)}, u32[]{:S(2)}) copy-start(bf16[1024,2048]{1,0:T(8,128)(2,1)} %param.17) | copy-start | bytes 12582916
  13.4 32.6 %copy-start.21 = (f32[1024]{0:T(1024)}, f32[1024]{0:T(1024)S(1)}, u32[]{:S(2)}) copy-start(f32[1024]{0:T(1024)S(1)} %get-tuple-element.221) | copy-start | bytes 12292
  23.8 22.1 %copy-start.19 = (f32[8,1,256]{2,1,0:T(1,128)}, f32[8,1,256]{2,1,0:T(1,128)S(1)}, u32[]{:S(2)}) copy-start(f32[8,1,256]{2,1,0:T(1,128)S(1)} %convert_element_type.218) | copy-start | bytes 24580
  24.8 39.6 %copy-start.12 = (f32[512,32]{0,1:T(8,128)}, f32[512,32]{0,1:T(8,128)S(1)}, u32[]{:S(2)}) copy-start(f32[512,32]{0,1:T(8,128)S(1)} %get-tuple-element.226) | copy-start | bytes 196612
  35.6 13.9 %copy-start.8 = (bf16[2048,64]{0,1:T(8,128)(2,1)}, bf16[2048,64]{0,1:T(8,128)(2,1)S(1)}, u32[]{:S(2)}) copy-start(bf16[2048,64]{0,1:T(8,128)(2,1)S(1)} %all_gather.29) | copy-start | bytes 786436
  44.9 4.5 copy-start.10
  46.0 2.0 copy-start.3
  83.7 6.3 copy-start.15
  90.0 1.8 copy-start.31
  90.0 1.8 copy-start.27
  90.1 199.3 %all-gather.14.cloned.1.call-start = ((), (), s32[]{:S(2)}) async-start(), calls=%async_computation.11 | async-start | bytes 6488064 | tf_op jit(solution)/shard_map/all_gather | solution.py:131
  90.6 243.6 %all-gather.12.cloned.1.call-start = ((), (), s32[]{:S(2)}) async-start(), calls=%async_computation.10 | async-start | bytes 6488064 | tf_op jit(solution)/shard_map/all_gather | solution.py:130
  91.2 289.1 %all-gather.16.cloned.1.call-start = ((), (), s32[]{:S(2)}) async-start(), calls=%async_computation.12 | async-start | bytes 6488064 | tf_op jit(solution)/shard_map/all_gather | solution.py:132
  91.8 480.3 %all-reduce.10.cloned.1.call-start = ((), (), s32[]{:S(2)}) async-start(), calls=%async_computation.13 | async-start | bytes 8388608 | tf_op jit(solution)/shard_map/psum | solution.py:194
  91.9 488.8 %copy-start.25 = (f32[1,4,2,128]{3,1,2,0:T(4,128)}, f32[1,4,2,128]{3,1,2,0:T(4,128)S(1)}, u32[]{:S(2)}) copy-start(f32[1,4,2,128]{3,1,2,0:T(4,128)S(1)} %copy.87) | copy-start | bytes 12292
  245.4 5.0 copy-start.1
  245.4 5.9 copy-start.4
  380.3 17.0 %copy-start.28 = (bf16[2048,1408]{1,0:T(8,128)(2,1)S(1)}, bf16[2048,1408]{1,0:T(8,128)(2,1)}, u32[]{:S(2)}) copy-start(bf16[2048,1408]{1,0:T(8,128)(2,1)} %all-gather.12.cloned.1.call-done) | copy-start | bytes 17301508
  397.3 8.7 copy-start.33
  417.0 324.9 %reduce-scatter.10.cloned.1.call-start = ((), (), s32[]{:S(2)}) async-start(), calls=%async_computation.15 | async-start | bytes 294912 | tf_op jit(solution)/shard_map/reduce_scatter | solution.py:254
  572.1 8.6 copy-start.2
  572.1 8.6 copy-start.5
  572.1 8.6 copy-start.7
  580.7 6.1 copy-start.30
  586.8 3.4 copy-start.6
  590.6 1.5 copy-start.13
  593.8 2.5 copy-start.14
  599.1 2.7 copy-start.17
  628.7 2.5 copy-start.14
  634.0 2.7 copy-start.17
  668.0 75.3 %reduce-scatter.12.cloned.1.call-start = ((), (), s32[]{:S(2)}) async-start(), calls=%async_computation.16 | async-start | bytes 294912 | tf_op jit(solution)/shard_map/reduce_scatter | solution.py:257
  674.7 107.7 %reduce-scatter.8.cloned.1.call-start = ((), (), s32[]{:S(2)}) async-start(), calls=%async_computation.14 | async-start | bytes 2359296 | tf_op jit(solution)/shard_map/reduce_scatter | solution.py:251
  674.7 6.1 copy-start.16
  680.8 146.0 %reduce-scatter.14.cloned.1.call-start = ((), (), s32[]{:S(2)}) async-start(), calls=%async_computation.17 | async-start | bytes 2359296 | tf_op jit(solution)/shard_map/reduce_scatter | solution.py:260
  687.9 201.2 %reduce-scatter.18.cloned.1.call-start = ((), (), s32[]{:S(2)}) async-start(), calls=%async_computation.19 | async-start | bytes 6488064 | tf_op jit(solution)/shard_map/reduce_scatter | solution.py:266
  699.0 252.6 %reduce-scatter.16.cloned.1.call-start = ((), (), s32[]{:S(2)}) async-start(), calls=%async_computation.18 | async-start | bytes 6488064 | tf_op jit(solution)/shard_map/reduce_scatter | solution.py:263
  710.1 303.8 %reduce-scatter.20.cloned.1.call-start = ((), (), s32[]{:S(2)}) async-start(), calls=%async_computation.20 | async-start | bytes 6488064 | tf_op jit(solution)/shard_map/reduce_scatter | solution.py:269
  721.6 11.2 copy-start.9
  721.6 586.1 %all-reduce.12.cloned.1.call-start = ((), (), s32[]{:S(2)}) async-start(), calls=%async_computation.21 | async-start | bytes 16777216 | tf_op jit(solution)/shard_map/psum | solution.py:177
  732.8 1.6 copy-start.29
  734.4 2.4 copy-start.11
  740.0 567.7 %copy-start.20 = (f32[8,1,256]{2,1,0:T(1,128)S(1)}, f32[8,1,256]{2,1,0:T(1,128)}, u32[]{:S(2)}) copy-start(f32[8,1,256]{2,1,0:T(1,128)} %copy-done.19) | copy-start | bytes 24580
  740.0 567.7 %copy-start.22 = (f32[1024]{0:T(1024)S(1)}, f32[1024]{0:T(1024)}, u32[]{:S(2)}) copy-start(f32[1024]{0:T(1024)} %copy-done.21) | copy-start | bytes 12292
  953.9 359.5 %copy-start.24 = (bf16[2048]{0:T(1024)(128)(2,1)S(1)}, bf16[2048]{0:T(1024)(128)(2,1)}, u32[]{:S(2)}) copy-start(bf16[2048]{0:T(1024)(128)(2,1)} %get-tuple-element.159) | copy-start | bytes 12292
  953.9 373.8 %copy-start.23 = (f32[1024]{0:T(1024)S(1)}, f32[1024]{0:T(1024)}, u32[]{:S(2)}) copy-start(f32[1024]{0:T(1024)} %get-tuple-element.220) | copy-start | bytes 12292
  (5 other events, 4.2 us)
Sparse Core Ops, SparseCore 0:
  9.9 30.9 all-gather.7
  42.7 28.2 all-gather.9
  90.2 155.1 all-reduce.7
  247.1 42.1 all-gather.13
  291.0 43.1 all-gather.11
  336.0 44.2 all-gather.15
  417.1 154.9 all-reduce.9
  668.1 32.6 reduce-scatter.9
  704.4 33.6 reduce-scatter.11
  741.2 41.0 reduce-scatter.7
  785.6 41.1 reduce-scatter.13
  830.1 59.0 reduce-scatter.17
  892.6 59.0 reduce-scatter.15
  954.9 58.8 reduce-scatter.19
  1016.9 290.8 all-reduce.11
where the time goes:
time: 1360 us; the launch traced here: 1350 us
  waiting for transfers between devices  957 us (70%)
  matrix products  177 us (13%)
  other arithmetic  83.6 us (6%)
  local copies, waits for them, and re-layouts  61.2 us (4%)
  blocking collectives  53 us (4%)
  between operations  15.5 us (1%)
    psum x1, waiting for transfers between devices, per_device(): lax.psum(mlp_partial.astype(jnp.bfloat16), 'mp').astype(jnp.float32)  292 us
    psum x1, waiting for transfers between devices, per_device(): lax.psum(partial_two.astype(jnp.bfloat16), 'mp').astype(jnp.float32)  155 us
    psum x1, waiting for transfers between devices, per_device(): lax.psum(attn_partial.astype(jnp.bfloat16), 'mp').astype(jnp.float32)  145 us
    reduce_scatter x1, waiting for transfers between devices, per_device(): lax.psum_scatter(grad_up_w.astype(jnp.bfloat16), 'dp', scatter_dimension=...  60.6 us
    reduce_scatter x1, waiting for transfers between devices, per_device(): lax.psum_scatter(grad_gate_w.astype(jnp.bfloat16), 'dp', scatter_dimensio...  60.2 us
    reduce_scatter x1, waiting for transfers between devices, per_device(): lax.psum_scatter(grad_down.astype(jnp.bfloat16), 'dp', scatter_dimension=...  59.9 us
    reduce_scatter x1, waiting for transfers between devices, per_device(): lax.psum_scatter(grad_out_w.astype(jnp.bfloat16), 'dp', scatter_dimension...  42.6 us
    dynamic_update_slice x4, local copies, waits for them, and re-layouts, per_device(): lax.map(backward_one, (query_rot, key_rot, value_rows, doc_ids, logsum, g...  41.4 us
  transfers between devices with their start and end apart: 15, of which 11 were waited for; matrix products, arithmetic and copies ran while one was open for 12% of the time, Pallas kernels for 0%

commit v1 on v0

--- a/solution.py
+++ b/solution.py
@@ -174,7 +174,10 @@
     hidden = (swish_gate * up_lin).astype(jnp.bfloat16)
     mlp_partial = jnp.dot(hidden, full_down, preferred_element_type=jnp.float32)
     output = (
-        hidden_in + lax.psum(mlp_partial.astype(jnp.bfloat16), "mp").astype(jnp.float32)
+        hidden_in
+        + jnp.sum(lax.all_gather(mlp_partial.astype(jnp.bfloat16), "mp"), axis=0).astype(
+            jnp.float32
+        )
     ).astype(jnp.bfloat16)
     grad_y = cotangent.astype(jnp.float32) * selection.reshape(tok_local, 1).astype(jnp.float32)
     grad_y_low = grad_y.astype(jnp.bfloat16)

time: 1360 us -> 1410 us (1.037)
  matrix products: 177 us -> 200 us
  waiting for transfers between devices: 957 us -> 972 us
    all_gather x0 -> x1, waiting for transfers between devices: none -> 280 us  [per_device(): lax.all_gather(mlp_partial.astype(jnp.bfloat16), 'mp')]
    psum x1, waiting for transfers between devices: 292 us -> 155 us  [per_device(): lax.psum(partial_one.astype(jnp.bfloat16), 'mp').astype(jnp.float32)]
    reduce_scatter x1, waiting for transfers between devices: 60.6 us -> 0.01 us  [per_device(): lax.psum_scatter(grad_up_w.astype(jnp.bfloat16), 'dp', scatter_dimension=...]
    reduce_scatter x1, waiting for transfers between devices: 60.2 us -> 0.02 us  [per_device(): lax.psum_scatter(grad_gate_w.astype(jnp.bfloat16), 'dp', scatter_dimensio...]
    psum x1, waiting for transfers between devices: 155 us -> 110 us  [per_device(): lax.psum(partial_two.astype(jnp.bfloat16), 'mp').astype(jnp.float32)]
    reduce_scatter x1, waiting for transfers between devices: 59.9 us -> 21.3 us  [per_device(): lax.psum_scatter(grad_down.astype(jnp.bfloat16), 'dp', scatter_dimension=...]
    reduce_scatter x1, waiting for transfers between devices: 0.01 us -> 35.3 us  [per_device(): lax.psum_scatter(grad_value_w.astype(jnp.bfloat16), 'dp', scatter_dimensi...]
    reduce_scatter x1, waiting for transfers between devices: 0.02 us -> 34.3 us  [per_device(): lax.psum_scatter(grad_key_w.astype(jnp.bfloat16), 'dp', scatter_dimension...]
  transfers between devices with their start and end apart: 15 -> 16, of which waited for: 11 -> 12; matrix products, arithmetic and copies ran while one was open for 12% -> 21% of each run, Pallas kernels for 0% -> 0%
where the time goes in v1:
time: 1410 us; the launch traced here: 1400 us
  waiting for transfers between devices  972 us (69%)
  matrix products  200 us (14%)
  other arithmetic  90.9 us (6%)
  local copies, waits for them, and re-layouts  63.9 us (5%)
  blocking collectives  51.5 us (4%)
  between operations  15.5 us (1%)
    all_gather x1, waiting for transfers between devices, per_device(): lax.all_gather(mlp_partial.astype(jnp.bfloat16), 'mp')  280 us
    psum x1, waiting for transfers between devices, per_device(): lax.psum(partial_one.astype(jnp.bfloat16), 'mp').astype(jnp.float32)  155 us
    psum x1, waiting for transfers between devices, per_device(): lax.psum(attn_partial.astype(jnp.bfloat16), 'mp').astype(jnp.float32)  145 us
    psum x1, waiting for transfers between devices, per_device(): lax.psum(partial_two.astype(jnp.bfloat16), 'mp').astype(jnp.float32)  110 us
    reduce_scatter x1, waiting for transfers between devices, per_device(): lax.psum_scatter(grad_out_w.astype(jnp.bfloat16), 'dp', scatter_dimension...  42.9 us
    reduce_scatter x1, waiting for transfers between devices, per_device(): lax.psum_scatter(grad_query_w.astype(jnp.bfloat16), 'dp', scatter_dimensi...  42.5 us
    dynamic_update_slice x4, local copies, waits for them, and re-layouts, per_device(): lax.map(backward_one, (query_rot, key_rot, value_rows, doc_ids, logsum, g...  41.4 us
    reduce_scatter x1, waiting for transfers between devices, per_device(): lax.psum_scatter(grad_value_w.astype(jnp.bfloat16), 'dp', scatter_dimensi...  35.3 us
  transfers between devices with their start and end apart: 16, of which 12 were waited for; matrix products, arithmetic and copies ran while one was open for 21% of the time, Pallas kernels for 0%

profile of v1, /device:TPU:0, one launch (start us, length us, event | category | flops | bytes accessed | tf_op | source)
XLA Modules:
  0.0 1395.2 jit_solution(2791962362640767073)
XLA Ops:
  13.2 10.4 all-gather.1
  23.7 9.8 all_gather.35
  39.2 9.1 all_gather.34
  52.9 6.6 fusion.89
  65.9 15.0 %while.26 = (s32[]{:T(128)}, bf16[2,512,512]{2,1,0:T(8,128)(2,1)S(1)}, f32[2,1,8,512,1]{3,2,4,1,0:T(8,128)}, bf16[2,512,1,64]{1,3,2,0:T(8,128)(2,1)S(1)}, s32[2,...) while((s32[]{:T(128)}, ...), condition=%wide.region_4.5_spmd, body=%wide.region_1.4_spmd.sunk | while | flops 562819072 | bytes 29630048 | solution.py:164
  81.0 6.7 convolution_convert_fusion.4
  89.6 8.5 all-gather.2
  98.1 144.9 %all-reduce.7.cloned.1.call-done = bf16[1024,2048]{1,0:T(8,128)(2,1)} async-done(((bf16[1024,2048]{1,0:T(8,128)(2,1)}), bf16[1024,2048]{1,0:T(8,128)(2,1)}) %all-reduce.7.cloned.1.call-update) | async-done | bytes 4194320 | tf_op jit(solution)/shard_map/psum | solution.py:167
  243.0 5.0 multiply_reduce_fusion
  248.9 4.2 multiply_convert_fusion
  253.1 33.8 %all-gather.14.cloned.1.call-done = bf16[2048,1408]{1,0:T(8,128)(2,1)} async-done(((bf16[256,1408]{1,0:T(8,128)(2,1)}), bf16[2048,1408]{1,0:T(8,128)(2,1)}) %all-gather.14.cloned.1.call-update) | async-done | bytes 5767184 | tf_op jit(solution)/shard_map/all_gather | solution.py:130
  286.9 11.7 fusion.90
  298.6 33.3 %all-gather.16.cloned.1.call-done = bf16[2048,1408]{1,0:T(8,128)(2,1)} async-done(((bf16[256,1408]{1,0:T(8,128)(2,1)}), bf16[2048,1408]{1,0:T(8,128)(2,1)}) %all-gather.16.cloned.1.call-update) | async-done | bytes 5767184 | tf_op jit(solution)/shard_map/all_gather | solution.py:131
  331.9 11.7 fusion.91
  343.6 34.3 %all-gather.18.cloned.1.call-done = bf16[1408,2048]{1,0:T(8,128)(2,1)} async-done(((bf16[1408,256]{1,0:T(8,128)(2,1)}), bf16[1408,2048]{1,0:T(8,128)(2,1)}) %all-gather.18.cloned.1.call-update) | async-done | bytes 5767184 | tf_op jit(solution)/shard_map/all_gather | solution.py:132
  377.9 14.7 %multiply_convert_fusion.1 = (bf16[1024,1408]{1,0:T(8,128)(2,1)S(1)}, bf16[1024,1408]{1,0:T(8,128)(2,1)S(1)}, bf16[1024,1408]{1,0:T(8,128)(2,1)S(1)}) fusion(f32[1024,1408]{1,0:T(8,128)} %fusion.90, f32[1024,1408]{1,0:T(8,128)} %fusion.91, bf16[1408,2048]{1,0:T(8,128)(2,1)} %all-gather.18.cloned.1.call-done, bf16[1024,2048]{1,0:T(8,128)(2,1)} %param.29, ...), kind=kOutput, calls=%fused_computation.103 | convolution fusion | flops 5933498368 | bytes 30150656 | tf_op jit(solution)/shard_map/td,fd->tf/dot_general | solution.py:185
  392.6 10.9 fusion.92
  403.5 8.5 add_convert_fusion.1
  412.1 11.0 convolution_convert_fusion.3
  423.1 11.0 convolution_convert_fusion.2
  434.2 11.0 convolution_convert_fusion.1
  445.2 11.6 convolution_convert_fusion
  456.9 110.3 %all-reduce.9.cloned.1.call-done = bf16[1024,2048]{1,0:T(8,128)(2,1)} async-done(((bf16[1024,2048]{1,0:T(8,128)(2,1)}), bf16[1024,2048]{1,0:T(8,128)(2,1)}) %all-reduce.9.cloned.1.call-update) | async-done | bytes 4194320 | tf_op jit(solution)/shard_map/psum | solution.py:197
  567.2 7.0 fusion.65
  574.2 280.3 %all-gather.20.cloned.1.call-done = bf16[4096,2048]{1,0:T(8,128)(2,1)} async-done(((bf16[1024,2048]{1,0:T(8,128)(2,1)}), bf16[4096,2048]{1,0:T(8,128)(2,1)}) %all-gather.20.cloned.1.call-update) | async-done | bytes 16777232 | tf_op jit(solution)/shard_map/all_gather | solution.py:178
  854.5 12.1 reduce_sum.86
  866.6 11.9 fusion.62
  882.4 98.6 %while.27 = (s32[]{:T(128)}, f32[2,512,8,64]{1,0,3,2:T(2,128)}, f32[2,512,1,64]{1,3,2,0:T(8,128)S(1)}, bf16[2,512,1,64]{1,3,2,0:T(8,128)(2,1)}, bf16[2,512,1,64]...) while((s32[]{:T(128)}, f32[2,512,8,64]{1,0,3,2:T(2,128)}, ...), condition=%wide.region_12.13_spmd, body=%wide.region_10.12_spmd.sunk | while | flops 1374711808 | bytes 120120048 | solution.py:212
  882.6 4.6 fusion.174
  889.1 5.0 fusion.176
  901.8 19.6 %dynamic_update_slice.32 = f32[2,512,8,64]{1,0,3,2:T(2,128)} dynamic-update-slice(f32[2,512,8,64]{1,0,3,2:T(2,128)} %get-tuple-element.376, f32[1,512,8,64]{1,0,3,2:T(1,128)S(1)} %copy.100, s32[]{:T(128)} %get-tuple-element.375, s32[]{:T(128)} %constant.67.clone.1..sunk, s32[]{:T(128)} %constant.67.clone.1..sunk, s32[]{:T(128)} %constant.67.clone.1..sunk) | dynamic-update-slice | bytes 2097156 | tf_op jit(solution)/shard_map/while/body/jit(dynamic_update_index_in_dim)/dynamic_update_slice | solution.py:212
  925.0 7.0 fusion.180
  932.0 4.6 fusion.174
  938.4 5.0 fusion.176
  951.9 19.6 %dynamic_update_slice.32 = f32[2,512,8,64]{1,0,3,2:T(2,128)} dynamic-update-slice(f32[2,512,8,64]{1,0,3,2:T(2,128)} %get-tuple-element.376, f32[1,512,8,64]{1,0,3,2:T(1,128)S(1)} %copy.100, s32[]{:T(128)} %get-tuple-element.375, s32[]{:T(128)} %constant.67.clone.1..sunk, s32[]{:T(128)} %constant.67.clone.1..sunk, s32[]{:T(128)} %constant.67.clone.1..sunk) | dynamic-update-slice | bytes 2097156 | tf_op jit(solution)/shard_map/while/body/jit(dynamic_update_index_in_dim)/dynamic_update_slice | solution.py:212
  975.1 5.9 fusion.180
  985.3 4.2 convolution_convert_fusion.7
  989.6 8.7 convolution_convert_fusion.5
  1001.3 3.9 convolution_convert_fusion.6
  1018.6 21.3 %reduce-scatter.20.cloned.1.call-done = bf16[1408,256]{1,0:T(8,128)(2,1)} async-done(((bf16[1408,2048]{1,0:T(8,128)(2,1)}), bf16[1408,256]{1,0:T(8,128)(2,1)}) %reduce-scatter.20.cloned.1.call-update) | async-done | bytes 720912 | tf_op jit(solution)/shard_map/reduce_scatter | solution.py:272
  1042.1 34.3 %reduce-scatter.10.cloned.1.call-done = bf16[256,64]{0,1:T(8,128)(2,1)} async-done(((bf16[2048,64]{0,1:T(8,128)(2,1)}), bf16[256,64]{0,1:T(8,128)(2,1)}) %reduce-scatter.10.cloned.1.call-update) | async-done | bytes 32784 | tf_op jit(solution)/shard_map/reduce_scatter | solution.py:257
  1077.8 35.3 %reduce-scatter.12.cloned.1.call-done = bf16[256,64]{0,1:T(8,128)(2,1)} async-done(((bf16[2048,64]{0,1:T(8,128)(2,1)}), bf16[256,64]{0,1:T(8,128)(2,1)}) %reduce-scatter.12.cloned.1.call-update) | async-done | bytes 32784 | tf_op jit(solution)/shard_map/reduce_scatter | solution.py:260
  1114.6 42.9 %reduce-scatter.14.cloned.1.call-done = bf16[512,256]{1,0:T(8,128)(2,1)} async-done(((bf16[512,2048]{1,0:T(8,128)(2,1)}), bf16[512,256]{1,0:T(8,128)(2,1)}) %reduce-scatter.14.cloned.1.call-update) | async-done | bytes 262160 | tf_op jit(solution)/shard_map/reduce_scatter | solution.py:263
  1159.2 42.5 %reduce-scatter.8.cloned.1.call-done = bf16[256,512]{1,0:T(8,128)(2,1)} async-done(((bf16[2048,512]{1,0:T(8,128)(2,1)}), bf16[256,512]{1,0:T(8,128)(2,1)}) %reduce-scatter.8.cloned.1.call-update) | async-done | bytes 262160 | tf_op jit(solution)/shard_map/reduce_scatter | solution.py:254
  1203.6 155.4 %all-reduce.11.cloned.1.call-done = bf16[1024,2048]{1,0:T(8,128)(2,1)} async-done(((bf16[1024,2048]{1,0:T(8,128)(2,1)}), bf16[1024,2048]{1,0:T(8,128)(2,1)}) %all-reduce.11.cloned.1.call-update) | async-done | bytes 4194320 | tf_op jit(solution)/shard_map/psum | solution.py:240
  1359.0 5.6 fusion.72
  1364.6 13.7 all-reduce.2
  1379.0 9.5 fusion.60
  (216 shorter events, 100.5 us)
Async XLA Ops:
  7.2 45.8 %all-gather.10.cloned.1.call-start = ((), (), s32[]{:S(2)}) async-start(), calls=%async_computation.7 | async-start | bytes 2359296 | tf_op jit(solution)/shard_map/all_gather | solution.py:126
  7.9 73.1 %all-gather.12.cloned.1.call-start = ((), (), s32[]{:S(2)}) async-start(), calls=%async_computation.8 | async-start | bytes 2359296 | tf_op jit(solution)/shard_map/all_gather | solution.py:129
  8.7 234.3 %all-reduce.7.cloned.1.call-start = ((), (), s32[]{:S(2)}) async-start(), calls=%async_computation.9 | async-start | bytes 8388608 | tf_op jit(solution)/shard_map/psum | solution.py:167
  8.7 24.8 %copy-start.1 = (bf16[1024,2048]{1,0:T(8,128)(2,1)S(1)}, bf16[1024,2048]{1,0:T(8,128)(2,1)}, u32[]{:S(2)}) copy-start(bf16[1024,2048]{1,0:T(8,128)(2,1)} %param.17) | copy-start | bytes 12582916
  12.6 21.9 %copy-start.26 = (f32[1024]{0:T(1024)}, f32[1024]{0:T(1024)S(1)}, u32[]{:S(2)}) copy-start(f32[1024]{0:T(1024)S(1)} %get-tuple-element.219) | copy-start | bytes 12292
  23.7 10.9 copy-start.24
  33.5 5.7 copy-start.28
  39.2 24.0 %copy-start.17 = (f32[512,32]{0,1:T(8,128)}, f32[512,32]{0,1:T(8,128)S(1)}, u32[]{:S(2)}) copy-start(f32[512,32]{0,1:T(8,128)S(1)} %get-tuple-element.224) | copy-start | bytes 196612
  80.9 6.8 copy-start.5
  80.9 6.8 copy-start.9
  80.9 6.8 copy-start.19
  81.0 6.8 copy-start.21
  87.8 10.3 copy-start.31
  87.8 199.1 %all-gather.14.cloned.1.call-start = ((), (), s32[]{:S(2)}) async-start(), calls=%async_computation.10 | async-start | bytes 6488064 | tf_op jit(solution)/shard_map/all_gather | solution.py:130
  88.4 243.5 %all-gather.16.cloned.1.call-start = ((), (), s32[]{:S(2)}) async-start(), calls=%async_computation.11 | async-start | bytes 6488064 | tf_op jit(solution)/shard_map/all_gather | solution.py:131
  89.0 288.9 %all-gather.18.cloned.1.call-start = ((), (), s32[]{:S(2)}) async-start(), calls=%async_computation.12 | async-start | bytes 6488064 | tf_op jit(solution)/shard_map/all_gather | solution.py:132
  89.5 477.6 %all-reduce.9.cloned.1.call-start = ((), (), s32[]{:S(2)}) async-start(), calls=%async_computation.13 | async-start | bytes 8388608 | tf_op jit(solution)/shard_map/psum | solution.py:197
  243.0 5.0 copy-start.2
  243.0 5.9 copy-start.8
  392.6 10.9 copy-start.37
  392.6 10.9 copy-start.38
  392.6 10.9 copy-start.32
  412.0 442.5 %all-gather.20.cloned.1.call-start = ((), (), s32[]{:S(2)}) async-start(), calls=%async_computation.22 | async-start | bytes 20971520 | tf_op jit(solution)/shard_map/all_gather | solution.py:178
  423.1 590.9 %reduce-scatter.16.cloned.1.call-start = ((), (), s32[]{:S(2)}) async-start(), calls=%async_computation.19 | async-start | bytes 6488064 | tf_op jit(solution)/shard_map/reduce_scatter | solution.py:266
  434.1 582.1 %reduce-scatter.18.cloned.1.call-start = ((), (), s32[]{:S(2)}) async-start(), calls=%async_computation.20 | async-start | bytes 6488064 | tf_op jit(solution)/shard_map/reduce_scatter | solution.py:269
  445.2 594.7 %reduce-scatter.20.cloned.1.call-start = ((), (), s32[]{:S(2)}) async-start(), calls=%async_computation.21 | async-start | bytes 6488064 | tf_op jit(solution)/shard_map/reduce_scatter | solution.py:272
  456.8 619.6 %reduce-scatter.10.cloned.1.call-start = ((), (), s32[]{:S(2)}) async-start(), calls=%async_computation.16 | async-start | bytes 294912 | tf_op jit(solution)/shard_map/reduce_scatter | solution.py:257
  866.6 11.9 copy-start.34
  878.5 3.9 copy-start.7
  882.4 98.6 %copy-start.18 = (f32[512,32]{0,1:T(8,128)S(1)}, f32[512,32]{0,1:T(8,128)}, u32[]{:S(2)}) copy-start(f32[512,32]{0,1:T(8,128)} %copy-done.17) | copy-start | bytes 196612
  882.4 98.6 %copy-start.22 = (f32[512,32]{0,1:T(8,128)S(1)}, f32[512,32]{0,1:T(8,128)}, u32[]{:S(2)}) copy-start(f32[512,32]{0,1:T(8,128)} %get-tuple-element.222) | copy-start | bytes 196612
  882.6 6.2 copy-start.11
  889.1 5.1 slice-start
  889.1 6.0 slice-start.1
  932.0 6.2 copy-start.11
  938.4 5.6 slice-start
  938.4 6.9 slice-start.1
  981.0 4.1 copy-start.23
  985.0 128.1 %reduce-scatter.12.cloned.1.call-start = ((), (), s32[]{:S(2)}) async-start(), calls=%async_computation.17 | async-start | bytes 294912 | tf_op jit(solution)/shard_map/reduce_scatter | solution.py:260
  989.5 9.1 copy-start.16
  989.5 168.0 %reduce-scatter.14.cloned.1.call-start = ((), (), s32[]{:S(2)}) async-start(), calls=%async_computation.18 | async-start | bytes 2359296 | tf_op jit(solution)/shard_map/reduce_scatter | solution.py:263
  998.3 203.4 %reduce-scatter.8.cloned.1.call-start = ((), (), s32[]{:S(2)}) async-start(), calls=%async_computation.15 | async-start | bytes 2359296 | tf_op jit(solution)/shard_map/reduce_scatter | solution.py:254
  1001.3 4.0 copy-start.13
  1005.3 353.7 %all-reduce.11.cloned.1.call-start = ((), (), s32[]{:S(2)}) async-start(), calls=%async_computation.14 | async-start | bytes 8388608 | tf_op jit(solution)/shard_map/psum | solution.py:240
  1012.6 346.4 %copy-start.25 = (f32[8,1,256]{2,1,0:T(1,128)S(1)}, f32[8,1,256]{2,1,0:T(1,128)}, u32[]{:S(2)}) copy-start(f32[8,1,256]{2,1,0:T(1,128)} %copy-done.24) | copy-start | bytes 24580
  1012.6 346.4 %copy-start.27 = (f32[1024]{0:T(1024)S(1)}, f32[1024]{0:T(1024)}, u32[]{:S(2)}) copy-start(f32[1024]{0:T(1024)} %copy-done.26) | copy-start | bytes 12292
  1018.6 346.1 %copy-start.30 = (bf16[2048]{0:T(1024)(128)(2,1)S(1)}, bf16[2048]{0:T(1024)(128)(2,1)}, u32[]{:S(2)}) copy-start(bf16[2048]{0:T(1024)(128)(2,1)} %get-tuple-element.159) | copy-start | bytes 12292
  1018.6 360.4 %copy-start.29 = (f32[1024]{0:T(1024)S(1)}, f32[1024]{0:T(1024)}, u32[]{:S(2)}) copy-start(f32[1024]{0:T(1024)} %get-tuple-element.218) | copy-start | bytes 12292
  (13 other events, 31.4 us)
Sparse Core Ops, SparseCore 0:
  9.9 30.4 all-gather.9
  42.3 28.0 all-gather.11
  87.9 155.0 all-reduce.6
  244.7 42.1 all-gather.13
  288.7 43.1 all-gather.15
  333.6 44.2 all-gather.17
  412.1 154.9 all-reduce.8
  568.7 285.7 all-gather.19
  857.9 57.1 reduce-scatter.15
  918.5 58.9 reduce-scatter.17
  980.9 58.8 reduce-scatter.19
  1042.7 33.6 reduce-scatter.9
  1079.5 33.6 reduce-scatter.11
  1116.3 41.1 reduce-scatter.13
  1160.6 41.1 reduce-scatter.7
  1204.0 154.9 all-reduce.10
